TPU v7x, 32 devices: a whole 2x2x4 slice. The times are simulated.
32 devices in a mesh: blk: 8 (over z, core), bond: 4 (over y, x).
Axes of the slice: x: 2, y: 2, z: 4, core: 2. Of those that a mesh axis runs over, the one named last changes fastest.
Arguments:
- iso: bfloat16 [8, 256, 256, 256], P('blk', None, 'bond'), may hold values from -0.03125 to 0.03125
- edge_left: bfloat16 [8, 256, 256], P('blk'), may hold values from -0.375 to 0.375
- edge_right: bfloat16 [8, 256, 256], P('blk'), may hold values from -0.375 to 0.375
- coupling: float32 [8, 256, 256], P('blk'), may hold values from -0.25 to 0.25
Outputs:
- iso_out: bfloat16 [8, 256, 256, 256], P('blk', None, 'bond')
- top_env: float32 [8, 256, 256], P('blk')
All inputs are finite; a program needn't handle non-finite values.
Results may differ from a plain program's by a relative error of at most 0.00105.
The roundings to bfloat16 on the way count: a program that leaves them out, or rounds other values in their place, can miss the bound.
Values may be sent and summed in bfloat16 or wider, within the bound.
A program may use at most 128 MiB of HBM per device.

v0:
```python
import jax
import jax.numpy as jnp
from jax import lax
from jax.experimental import pallas as pl
from jax.experimental.pallas import tpu as pltpu
from jax.sharding import PartitionSpec as P

NEWTON = 2
CHUNK = 16

highest = lax.Precision.HIGHEST
f32 = jnp.float32
bf16 = jnp.bfloat16


def shifted(block, axis, distance):
    devices = range(lax.axis_size(axis))
    route = [((i - distance) % len(devices), i) for i in devices]
    return lax.ppermute(block, axis, route)


def partner_2(block, axis, stride):
    count = lax.axis_size(axis)
    route = []
    for low in range(count):
        high = low | 1 << stride
        if high != low and high < count:
            route += [(low, high), (high, low)]
    return lax.ppermute(block, axis, route)


def mm(a, b):
    return jnp.dot(a, b, preferred_element_type=f32)


def tmm(a, b):
    return lax.dot_general(a, b, (((0,), (0,)), ((), ())), preferred_element_type=f32)


def ascend_kernel(iso_ref, edges_ref, rows_ref, total_ref):
    @pl.when(pl.program_id(0) == 0)
    def _():
        total_ref[...] = jnp.zeros_like(total_ref)

    chi = iso_ref.shape[0]
    rows_ref[...] = jnp.transpose(iso_ref[...], (1, 0, 2))

    def step(b, carry):
        one = rows_ref[b]
        for k in range(2):
            mapped = mm(edges_ref[k], one)
            high = mapped.astype(bf16)
            low = (mapped - high.astype(f32)).astype(bf16)
            total_ref[k] += tmm(one, high) + tmm(one, low)
        return carry

    lax.fori_loop(0, rows_ref.shape[0], step, 0, unroll=4)


def gram_kernel(rows_ref, mix_ref, top_ref, gram_ref):
    @pl.when(pl.program_id(0) == 0)
    def _():
        gram_ref[...] = jnp.zeros_like(gram_ref)

    def step(b, carry):
        one = rows_ref[b]
        grad = (mm(mix_ref[...], one) + mm(one, top_ref[...])).astype(bf16)
        gram_ref[...] += tmm(grad, grad)
        return carry

    lax.fori_loop(0, rows_ref.shape[0], step, 0, unroll=4)


def update_kernel(rows_ref, mix_ref, top_ref, rest_ref, mean_ref, out_ref, held_ref):
    mean = mean_ref[0, 0]

    def step(b, carry):
        one = rows_ref[b]
        grad = mm(mix_ref[...], one) + mm(one, top_ref[...])
        held_ref[b] = (mean * grad + mm(grad.astype(bf16), rest_ref[...])).astype(bf16)
        return carry

    lax.fori_loop(0, rows_ref.shape[0], step, 0, unroll=4)
    out_ref[...] = jnp.transpose(held_ref[...], (1, 0, 2))


def whole(shape):
    return pl.BlockSpec(shape, lambda i: (0,) * len(shape))


def body(iso, edge_left, edge_right, coupling):
    iso = iso[0]
    chi, depth, _ = iso.shape
    chunk = CHUNK if depth % CHUNK == 0 else depth
    steps = depth // chunk
    square = (chi, chi)
    iso_spec = pl.BlockSpec((chi, chunk, chi), lambda i: (0, i, 0))
    rows_spec = pl.BlockSpec((chunk, chi, chi), lambda i: (i, 0, 0))
    params = pltpu.CompilerParams(
        dimension_semantics=("arbitrary",), vmem_limit_bytes=48 * 1024 * 1024
    )
    work = 2 * depth * chi**3
    edges = jnp.stack([edge_left[0], edge_right[0]])
    rows, partial_value = pl.pallas_call(
        ascend_kernel,
        grid=(steps,),
        in_specs=[iso_spec, whole((2, *square))],
        out_specs=[rows_spec, whole((2, *square))],
        out_shape=[
            jax.ShapeDtypeStruct((depth, *square), bf16),
            jax.ShapeDtypeStruct((2, *square), f32),
        ],
        compiler_params=params,
        cost_estimate=pl.CostEstimate(flops=6 * work, bytes_accessed=4 * iso.size, transcendentals=0),
        name="ascend",
    )(iso, edges)
    ranks = lax.axis_size("bond")
    pieces = partial_value.reshape(ranks, -1, chi)
    pieces = lax.all_to_all(pieces, "bond", 0, 0, tiled=True)
    piece = jnp.sum(pieces, axis=0).astype(bf16)
    bounds = lax.all_gather(piece, "bond", axis=0, tiled=True).reshape(2, *square)
    own_left = bounds[0]
    own_right = bounds[1]
    from_left = shifted(own_right, "blk", 1)
    from_right = shifted(own_left, "blk", -1)
    environ = own_left.astype(f32) + own_right.astype(f32)
    couple_mat = coupling[0]
    for level_idx in range(lax.axis_size("blk").bit_length() - 1):
        partner = partner_2(environ, "blk", level_idx)
        carried = jnp.dot(
            jnp.dot(couple_mat, partner, precision=highest), couple_mat.T, precision=highest
        )
        environ = 0.5 * (environ + carried)
    top_low = environ.astype(bf16)
    mixed_op = edge_left[0].astype(f32) + from_left.astype(f32) + from_right.astype(f32)
    mixed_op = mixed_op.astype(bf16)
    part_gram = pl.pallas_call(
        gram_kernel,
        grid=(steps,),
        in_specs=[rows_spec, whole(square), whole(square)],
        out_specs=whole(square),
        out_shape=jax.ShapeDtypeStruct(square, f32),
        compiler_params=params,
        cost_estimate=pl.CostEstimate(flops=3 * work, bytes_accessed=2 * iso.size, transcendentals=0),
        name="gram",
    )(rows, mixed_op, top_low)
    left = jnp.trace(part_gram)
    extra = []
    for _ in range(3):
        head = lax.reduce_precision(left, 8, 7)
        extra.append(jnp.full((1, chi), head, f32))
        left = left - head
    packed = jnp.concatenate([part_gram, *extra, jnp.zeros((13, chi), f32)], axis=0).astype(bf16)
    packed = lax.all_gather(packed, "bond", axis=0).astype(f32)
    packed = jnp.sum(packed, axis=0)
    squares = packed[chi, 0] + packed[chi + 1, 0] + packed[chi + 2, 0]
    scale = lax.rsqrt(squares + 1e-06)
    first_gram = packed[:chi] * (scale * scale)
    gram = first_gram
    eye = jnp.eye(chi, dtype=f32)
    total = eye
    for newton_step in range(NEWTON):
        step = 1.5 * eye - 0.5 * gram
        total = step if newton_step == 0 else jnp.dot(total, step, precision=highest)
        if newton_step + 1 < NEWTON:
            gram = jnp.dot(jnp.dot(step, gram, precision=highest), step, precision=highest)
    mean = jnp.sum(first_gram * total) / jnp.maximum(jnp.trace(first_gram), 1e-30)
    rest = ((total - mean * eye) * scale).astype(bf16)
    updated = pl.pallas_call(
        update_kernel,
        grid=(steps,),
        in_specs=[
            rows_spec,
            whole(square),
            whole(square),
            whole(square),
            pl.BlockSpec(memory_space=pltpu.SMEM),
        ],
        out_specs=iso_spec,
        out_shape=jax.ShapeDtypeStruct(iso.shape, bf16),
        scratch_shapes=[pltpu.VMEM((chunk, *square), bf16)],
        compiler_params=params,
        cost_estimate=pl.CostEstimate(flops=3 * work, bytes_accessed=4 * iso.size, transcendentals=0),
        name="update",
    )(rows, mixed_op, top_low, rest, (mean * scale).reshape(1, 1))
    return (updated[None], environ[None])


def solution(mesh):
    placed = (
        P("blk", None, "bond", None),
        P("blk", None, None),
        P("blk", None, None),
        P("blk", None, None),
    )
    return jax.shard_map(
        body,
        mesh=mesh,
        in_specs=placed,
        out_specs=(P("blk", None, "bond", None), P("blk", None, None)),
        check_vma=False,
    )
```

profile of v0, /device:TPU:0, one launch (start us, length us, event | category | flops | bytes accessed | tf_op | source)
XLA Modules:
  0.0 146.4 jit_solution(3609040322086297706)
XLA Ops:
  0.6 0.0 copy-start
  0.6 1.0 pad_maximum_fusion.edges_ref
  1.7 0.0 copy-start.1
  1.7 29.8 %ascend.1 = (bf16[64,256,256]{2,1,0:T(8,128)(2,1)}, f32[2,256,256]{2,1,0:T(8,128)S(1)}) custom-call(bf16[256,64,256]{2,1,0:T(8,128)(2,1)} %bitcast.36, bf16[2,256,256]{2,1,0:T(8,128)(2,1)S(1)} %pad_maximum_fusion.edges_ref), custom_call_target="tpu_custom_call" | custom-call | flops 12884901888 | bytes 16777216 | tf_op jit(solution)/shard_map/ascend/pallas_call | solution.py:104
  31.5 13.5 %all_to_all.5 = f32[4,128,256]{2,1,0:T(8,128)S(1)} all-to-all(f32[4,128,256]{2,1,0:T(8,128)S(1)} %bitcast.34), channel_id=1, replica_groups=mesh['blk'=8,'bond'=4] {'bond'}, dimensions={0} | all-to-all | bytes 1048576 | tf_op jit(solution)/shard_map/all_to_all | solution.py:119
  45.1 8.6 %all_gather.7 = bf16[512,256]{1,0:T(8,128)(2,1)S(1)} all-gather(bf16[128,256]{1,0:T(8,128)(2,1)S(1)} %reduce_sum.43), channel_id=1, replica_groups=mesh['blk'=8,'bond'=4] {'bond'}, dimensions={0}, use_global_device_ids=true | all-gather | bytes 327680 | tf_op jit(solution)/shard_map/all_gather | solution.py:121
  53.7 0.1 collective-permute-start.2
  53.8 1.5 %collective-permute-done.2 = f32[256,256]{1,0:T(8,128)S(1)} collective-permute-done((f32[256,256]{1,0:T(8,128)S(1)}, f32[256,256]{1,0:T(8,128)S(1)}, u32[]{:S(2)}, u32[]{:S(2)}) %collective-permute-start.2) | collective-permute-done | bytes 262176 | tf_op jit(solution)/shard_map/ppermute | solution.py:29
  55.3 0.0 copy-done
  55.3 0.6 fusion.13
  55.9 0.6 fusion.3
  56.5 1.7 %collective-permute-start.3 = (f32[256,256]{1,0:T(8,128)S(1)}, f32[256,256]{1,0:T(8,128)S(1)}, u32[]{:S(2)}, u32[]{:S(2)}) collective-permute-start(f32[256,256]{1,0:T(8,128)S(1)} %fusion.3), channel_id=1, source_target_pairs={{0,8},{8,0},{4,12},{12,4},{16,24},{24,16},{20,28},{28,20},{1,9},{9... | collective-permute-start | bytes 786440 | tf_op jit(solution)/shard_map/ppermute | solution.py:29
  58.2 0.1 collective-permute-start
  58.3 3.5 %collective-permute-start.1 = (bf16[256,256]{1,0:T(8,128)(2,1)S(1)}, bf16[256,256]{1,0:T(8,128)(2,1)S(1)}, u32[]{:S(2)}, u32[]{:S(2)}) collective-permute-start(bf16[256,256]{1,0:T(8,128)(2,1)S(1)} %get-tuple-element.14), channel_id=1, source_target_pairs={{4,0},{8,4},{12,8},{16,12},{20,16},{24,20},{28,24},{0,28},{5,1},{9... | collective-permute-start | bytes 393224 | tf_op jit(solution)/shard_map/ppermute | solution.py:19
  61.8 3.1 %collective-permute-done.3 = f32[256,256]{1,0:T(8,128)S(1)} collective-permute-done((f32[256,256]{1,0:T(8,128)S(1)}, f32[256,256]{1,0:T(8,128)S(1)}, u32[]{:S(2)}, u32[]{:S(2)}) %collective-permute-start.3) | collective-permute-done | bytes 262176 | tf_op jit(solution)/shard_map/ppermute | solution.py:29
  64.9 0.6 fusion.10
  65.5 0.6 fusion.2
  66.1 3.5 %collective-permute-start.4 = (f32[256,256]{1,0:T(8,128)S(1)}, f32[256,256]{1,0:T(8,128)S(1)}, u32[]{:S(2)}, u32[]{:S(2)}) collective-permute-start(f32[256,256]{1,0:T(8,128)S(1)} %fusion.2), channel_id=1, source_target_pairs={{0,16},{16,0},{4,20},{20,4},{8,24},{24,8},{12,28},{28,12},{1,17},{... | collective-permute-start | bytes 786440 | tf_op jit(solution)/shard_map/ppermute | solution.py:29
  69.6 0.0 collective-permute-done
  69.7 0.0 collective-permute-done.1
  69.7 0.0 copy-done.1
  69.7 0.1 fusion.5.mix_ref
  69.7 10.5 %collective-permute-done.4 = f32[256,256]{1,0:T(8,128)S(1)} collective-permute-done((f32[256,256]{1,0:T(8,128)S(1)}, f32[256,256]{1,0:T(8,128)S(1)}, u32[]{:S(2)}, u32[]{:S(2)}) %collective-permute-start.4) | collective-permute-done | bytes 262176 | tf_op jit(solution)/shard_map/ppermute | solution.py:29
  80.2 0.6 fusion.7
  80.8 1.3 fusion.40
  82.1 17.7 %gram.1 = f32[256,256]{1,0:T(8,128)S(1)} custom-call(bf16[64,256,256]{2,1,0:T(8,128)(2,1)} %get-tuple-element.4.rows_ref, bf16[256,256]{1,0:T(8,128)(2,1)S(1)} %fusion.5.mix_ref, bf16[256,256]{1,0:T(8,128)(2,1)S(1)} %get-tuple-element.15.top_ref), custom_call_target="tpu_custom_call" | custom-call | flops 6442450944 | bytes 8388608 | tf_op jit(solution)/shard_map/gram/pallas_call | solution.py:137
  99.8 0.6 select_reduce_fusion.1
  105.7 0.6 broadcast_in_dim.23
  106.4 0.2 concatenate.14
  106.5 10.5 %all_gather.8 = bf16[4,272,256]{2,1,0:T(8,128)(2,1)S(1)} all-gather(bf16[1,272,256]{2,1,0:T(8,128)(2,1)S(1)} %concatenate.14), channel_id=1, replica_groups=mesh['blk'=8,'bond'=4] {'bond'}, dimensions={0}, use_global_device_ids=true | all-gather | bytes 696320 | tf_op jit(solution)/shard_map/all_gather | solution.py:154
  117.0 0.1 convert_reduce_fusion
  117.1 0.5 fusion.38
  119.5 0.4 fusion.16
  120.0 0.4 fusion
  120.4 1.0 select_reduce_fusion
  122.7 23.7 %update.1 = bf16[256,64,256]{2,1,0:T(8,128)(2,1)} custom-call(bf16[64,256,256]{2,1,0:T(8,128)(2,1)} %get-tuple-element.4.rows_ref, bf16[256,256]{1,0:T(8,128)(2,1)S(1)} %fusion.5.mix_ref, bf16[256,256]{1,0:T(8,128)(2,1)S(1)} %get-tuple-element.15.top_ref, bf16[256,256]{1,0:T(8,128)(2,1)S(1)} %multiply_convert_fusion.rest_ref, f32[1,1]{1,0:T(1,128)} %bitcast.6.mean_ref), custom_call_target="tpu_custom_call" | custom-call | flops 6442450944 | bytes 16777216 | tf_op jit(solution)/shard_map/update/pallas_call | solution.py:169
  (7 shorter events, 0.1 us)
Async XLA Ops:
  0.6 54.7 %copy-start = (f32[1,256,256]{2,1,0:T(8,128)S(1)}, f32[1,256,256]{2,1,0:T(8,128)}, u32[]{:S(2)}) copy-start(f32[1,256,256]{2,1,0:T(8,128)} %param.7) | copy-start | bytes 786436
  1.7 68.0 %copy-start.1 = (bf16[1,256,256]{2,1,0:T(8,128)(2,1)S(1)}, bf16[1,256,256]{2,1,0:T(8,128)(2,1)}, u32[]{:S(2)}) copy-start(bf16[1,256,256]{2,1,0:T(8,128)(2,1)} %param.5) | copy-start | bytes 393220
  53.7 1.6 %collective-permute-start.2 = (f32[256,256]{1,0:T(8,128)S(1)}, f32[256,256]{1,0:T(8,128)S(1)}, u32[]{:S(2)}, u32[]{:S(2)}) collective-permute-start(f32[256,256]{1,0:T(8,128)S(1)} %convert_add_fusion.1), channel_id=1, source_target_pairs={{0,4},{4,0},{8,12},{12,8},{16,20},{20,16},{24,28},{28,24},{1,5},{5... | collective-permute-start | bytes 786440 | tf_op jit(solution)/shard_map/ppermute | solution.py:29
  56.5 8.4 %collective-permute-start.3 = (f32[256,256]{1,0:T(8,128)S(1)}, f32[256,256]{1,0:T(8,128)S(1)}, u32[]{:S(2)}, u32[]{:S(2)}) collective-permute-start(f32[256,256]{1,0:T(8,128)S(1)} %fusion.3), channel_id=1, source_target_pairs={{0,8},{8,0},{4,12},{12,4},{16,24},{24,16},{20,28},{28,20},{1,9},{9... | collective-permute-start | bytes 786440 | tf_op jit(solution)/shard_map/ppermute | solution.py:29
  58.2 11.5 %collective-permute-start = (bf16[256,256]{1,0:T(8,128)(2,1)S(1)}, bf16[256,256]{1,0:T(8,128)(2,1)S(1)}, u32[]{:S(2)}, u32[]{:S(2)}) collective-permute-start(bf16[256,256]{1,0:T(8,128)(2,1)S(1)} %get-tuple-element.13), channel_id=1, source_target_pairs={{28,0},{0,4},{4,8},{8,12},{12,16},{16,20},{20,24},{24,28},{29,1},{... | collective-permute-start | bytes 393224 | tf_op jit(solution)/shard_map/ppermute | solution.py:19
  58.3 11.4 %collective-permute-start.1 = (bf16[256,256]{1,0:T(8,128)(2,1)S(1)}, bf16[256,256]{1,0:T(8,128)(2,1)S(1)}, u32[]{:S(2)}, u32[]{:S(2)}) collective-permute-start(bf16[256,256]{1,0:T(8,128)(2,1)S(1)} %get-tuple-element.14), channel_id=1, source_target_pairs={{4,0},{8,4},{12,8},{16,12},{20,16},{24,20},{28,24},{0,28},{5,1},{9... | collective-permute-start | bytes 393224 | tf_op jit(solution)/shard_map/ppermute | solution.py:19
  66.1 14.1 %collective-permute-start.4 = (f32[256,256]{1,0:T(8,128)S(1)}, f32[256,256]{1,0:T(8,128)S(1)}, u32[]{:S(2)}, u32[]{:S(2)}) collective-permute-start(f32[256,256]{1,0:T(8,128)S(1)} %fusion.2), channel_id=1, source_target_pairs={{0,16},{16,0},{4,20},{20,4},{8,24},{24,8},{12,28},{28,12},{1,17},{... | collective-permute-start | bytes 786440 | tf_op jit(solution)/shard_map/ppermute | solution.py:29
where the time goes:
time: 147 us; the launch traced here: 146 us
  Pallas kernels  71.3 us (49%)
  blocking collectives  32.6 us (22%)
  waiting for transfers between devices  15.1 us (10%)
  between operations  9.12 us (6%)
  starting transfers between devices  8.84 us (6%)
  matrix products  6.14 us (4%)
  other arithmetic  1.9 us (1%)
    pallas_call x1, Pallas kernels, body(): pl.pallas_call(ascend_kernel, grid=(steps,), in_specs=[iso_spec, whole((2...  29.8 us
    pallas_call x1, Pallas kernels, body(): pl.pallas_call(update_kernel, grid=(steps,), in_specs=[rows_spec, whole(s...  23.7 us
    pallas_call x1, Pallas kernels, body(): pl.pallas_call(gram_kernel, grid=(steps,), in_specs=[rows_spec, whole(squ...  17.7 us
    ppermute x3, waiting for transfers between devices, partner_2(): return lax.ppermute(block, axis, route)  15.1 us
    all_to_all x1, blocking collectives, body(): pieces = lax.all_to_all(pieces, 'bond', 0, 0, tiled=True)  13.5 us
    all_gather x1, blocking collectives, body(): packed = lax.all_gather(packed, 'bond', axis=0).astype(f32)  10.5 us
    all_gather x1, blocking collectives, body(): lax.all_gather(piece, 'bond', axis=0, tiled=True).reshape(2, *square)  8.58 us
    ppermute x3, starting transfers between devices, partner_2(): return lax.ppermute(block, axis, route)  5.25 us
  transfers between devices with their start and end apart: 5, of which 3 were waited for; matrix products, arithmetic and copies ran while one was open for 1% of the time, Pallas kernels for 0%

commit v1 on v0

v1 whole, which is shorter than its diff:
```python
import jax
import jax.numpy as jnp
from jax import lax
from jax.experimental import pallas as pl
from jax.experimental.pallas import tpu as pltpu
from jax.sharding import PartitionSpec as P

NEWTON = 2
CHUNK = 16
GROUP = 4
TAIL = 16

highest = lax.Precision.HIGHEST
f32 = jnp.float32
bf16 = jnp.bfloat16


def shifted(block, axis, distance):
    devices = range(lax.axis_size(axis))
    route = [((i - distance) % len(devices), i) for i in devices]
    return lax.ppermute(block, axis, route)


def partner_2(block, axis, stride):
    count = lax.axis_size(axis)
    route = []
    for low in range(count):
        high = low | 1 << stride
        if high != low and high < count:
            route += [(low, high), (high, low)]
    return lax.ppermute(block, axis, route)


def mm(a, b):
    return jnp.dot(a, b, preferred_element_type=f32)


def ascend_kernel(iso_ref, edges_ref, rows_ref, total_ref):
    @pl.when(pl.program_id(0) == 0)
    def _():
        total_ref[...] = jnp.zeros_like(total_ref)

    chi = iso_ref.shape[0]
    rows_ref[...] = jnp.transpose(iso_ref[...], (1, 0, 2))

    def step(g, carry):
        mats = [rows_ref[g * GROUP + j] for j in range(GROUP)]
        turned = jnp.concatenate(mats, axis=0).T
        mapped = [mm(edges_ref[...], one) for one in mats]
        for k in range(2):
            both = jnp.concatenate([part[k * chi : (k + 1) * chi] for part in mapped], axis=0)
            high = both.astype(bf16)
            low = (both - high.astype(f32)).astype(bf16)
            total_ref[k] += mm(turned, high) + mm(turned, low)
        return carry

    lax.fori_loop(0, rows_ref.shape[0] // GROUP, step, 0, unroll=2)


def gram_kernel(rows_ref, mix_ref, self_ref, cross_ref, plain_ref):
    @pl.when(pl.program_id(0) == 0)
    def _():
        for ref in (self_ref, cross_ref, plain_ref):
            ref[...] = jnp.zeros_like(ref)

    def step(g, carry):
        mats = [rows_ref[g * GROUP + j] for j in range(GROUP)]
        rows = jnp.concatenate(mats, axis=0)
        moved = jnp.concatenate([mm(mix_ref[...], one).astype(bf16) for one in mats], axis=0)
        turned = moved.T
        self_ref[...] += mm(turned, moved)
        cross_ref[...] += mm(turned, rows)
        plain_ref[...] += mm(rows.T, rows)
        return carry

    lax.fori_loop(0, rows_ref.shape[0] // GROUP, step, 0, unroll=2)


def exact(a, b):
    return jnp.dot(a, b, precision=highest, preferred_element_type=f32)


def diagonal(shape):
    return lax.broadcasted_iota(jnp.int32, shape, 0) == lax.broadcasted_iota(jnp.int32, shape, 1)


def join_kernel(self_ref, cross_ref, plain_ref, top_ref, packed_ref):
    chi = self_ref.shape[0]
    top = top_ref[...].astype(f32)
    half = exact(cross_ref[...] + 0.5 * exact(top.T, plain_ref[...]), top)
    gram = self_ref[...] + half + half.T
    packed_ref[0:chi, :] = gram.astype(bf16)
    trace = jnp.sum(jnp.where(diagonal(gram.shape), gram, 0.0), keepdims=True)
    left = jnp.broadcast_to(trace, (TAIL, chi))
    place = lax.broadcasted_iota(jnp.int32, (TAIL, chi), 0)
    tail = jnp.zeros((TAIL, chi), f32)
    for row in range(3):
        head = left.astype(bf16).astype(f32)
        tail = jnp.where(place == row, head, tail)
        left = left - head
    packed_ref[chi : chi + TAIL, :] = tail.astype(bf16)


def update_kernel(rows_ref, mix_ref, top_ref, packed_ref, out_ref, held_ref, rest_ref, mean_ref):
    @pl.when(pl.program_id(0) == 0)
    def _():
        chi = mix_ref.shape[0]
        packed = packed_ref[0].astype(f32)
        for rank in range(1, packed_ref.shape[0]):
            packed = packed + packed_ref[rank].astype(f32)
        squares = jnp.sum(packed[chi:], axis=0, keepdims=True)
        scale = lax.rsqrt(squares + 1e-06)
        first_gram = packed[:chi] * (scale * scale)
        gram = first_gram
        eye = diagonal(gram.shape).astype(f32)
        total = eye
        for newton_step in range(NEWTON):
            step = 1.5 * eye - 0.5 * gram
            total = step if newton_step == 0 else exact(total, step)
            if newton_step + 1 < NEWTON:
                gram = exact(exact(step, gram), step)
        energy = jnp.sum(first_gram * eye, keepdims=True)
        mean = jnp.sum(first_gram * total, keepdims=True) / jnp.maximum(energy, 1e-30)
        rest_ref[...] = ((total - mean * eye) * scale).astype(bf16)
        mean_ref[...] = mean * scale

    mean = mean_ref[...]

    def step(g, carry):
        mats = [rows_ref[g * GROUP + j] for j in range(GROUP)]
        rows = jnp.concatenate(mats, axis=0)
        moved = jnp.concatenate([mm(mix_ref[...], one) for one in mats], axis=0)
        grad = moved + mm(rows, top_ref[...])
        done = (mean * grad + mm(grad.astype(bf16), rest_ref[...])).astype(bf16)
        held_ref[pl.ds(g * GROUP, GROUP)] = done.reshape(GROUP, *mix_ref.shape)
        return carry

    lax.fori_loop(0, rows_ref.shape[0] // GROUP, step, 0, unroll=2)
    out_ref[...] = jnp.transpose(held_ref[...], (1, 0, 2))


def whole(shape):
    return pl.BlockSpec(shape, lambda i: (0,) * len(shape))


def body(iso, edge_left, edge_right, coupling):
    iso = iso[0]
    chi, depth, _ = iso.shape
    chunk = CHUNK if depth % CHUNK == 0 else depth
    steps = depth // chunk
    square = (chi, chi)
    iso_spec = pl.BlockSpec((chi, chunk, chi), lambda i: (0, i, 0))
    rows_spec = pl.BlockSpec((chunk, chi, chi), lambda i: (i, 0, 0))
    params = pltpu.CompilerParams(
        dimension_semantics=("arbitrary",), vmem_limit_bytes=48 * 1024 * 1024
    )
    work = 2 * depth * chi**3
    edges = jnp.concatenate([edge_left[0], edge_right[0]], axis=0)
    rows, partial_value = pl.pallas_call(
        ascend_kernel,
        grid=(steps,),
        in_specs=[iso_spec, whole((2 * chi, chi))],
        out_specs=[rows_spec, whole((2, *square))],
        out_shape=[
            jax.ShapeDtypeStruct((depth, *square), bf16),
            jax.ShapeDtypeStruct((2, *square), f32),
        ],
        compiler_params=params,
        cost_estimate=pl.CostEstimate(flops=6 * work, bytes_accessed=4 * iso.size, transcendentals=0),
        name="ascend",
    )(iso, edges)
    ranks = lax.axis_size("bond")
    pieces = partial_value.reshape(ranks, -1, chi)
    pieces = lax.all_to_all(pieces, "bond", 0, 0, tiled=True)
    piece = jnp.sum(pieces, axis=0).astype(bf16)
    bounds = lax.all_gather(piece, "bond", axis=0, tiled=True).reshape(2, *square)
    own_left = bounds[0]
    own_right = bounds[1]
    from_left = shifted(own_right, "blk", 1)
    from_right = shifted(own_left, "blk", -1)
    mixed_op = edge_left[0].astype(f32) + from_left.astype(f32) + from_right.astype(f32)
    mixed_op = mixed_op.astype(bf16)
    environ = own_left.astype(f32) + own_right.astype(f32)
    couple_mat = coupling[0]
    levels = lax.axis_size("blk").bit_length() - 1
    for level_idx in range(levels):
        if level_idx == levels - 1:
            environ, mixed_op = lax.optimization_barrier((environ, mixed_op))
        partner = partner_2(environ, "blk", level_idx)
        carried = jnp.dot(
            jnp.dot(couple_mat, partner, precision=highest), couple_mat.T, precision=highest
        )
        environ = 0.5 * (environ + carried)
    grams = pl.pallas_call(
        gram_kernel,
        grid=(steps,),
        in_specs=[rows_spec, whole(square)],
        out_specs=[whole(square)] * 3,
        out_shape=[jax.ShapeDtypeStruct(square, f32)] * 3,
        compiler_params=params,
        cost_estimate=pl.CostEstimate(flops=4 * work, bytes_accessed=2 * iso.size, transcendentals=0),
        name="gram",
    )(rows, mixed_op)
    top_low = environ.astype(bf16)
    packed = pl.pallas_call(
        join_kernel,
        out_shape=jax.ShapeDtypeStruct((chi + TAIL, chi), bf16),
        compiler_params=pltpu.CompilerParams(vmem_limit_bytes=8 * 1024 * 1024),
        name="join",
    )(*grams, top_low)
    packed = lax.all_gather(packed, "bond", axis=0)
    updated = pl.pallas_call(
        update_kernel,
        grid=(steps,),
        in_specs=[rows_spec, whole(square), whole(square), whole(packed.shape)],
        out_specs=iso_spec,
        out_shape=jax.ShapeDtypeStruct(iso.shape, bf16),
        scratch_shapes=[
            pltpu.VMEM((chunk, *square), bf16),
            pltpu.VMEM(square, bf16),
            pltpu.VMEM((1, chi), f32),
        ],
        compiler_params=params,
        cost_estimate=pl.CostEstimate(flops=3 * work, bytes_accessed=4 * iso.size, transcendentals=0),
        name="update",
    )(rows, mixed_op, top_low, packed)
    return (updated[None], environ[None])


def solution(mesh):
    placed = (
        P("blk", None, "bond", None),
        P("blk", None, None),
        P("blk", None, None),
        P("blk", None, None),
    )
    return jax.shard_map(
        body,
        mesh=mesh,
        in_specs=placed,
        out_specs=(P("blk", None, "bond", None), P("blk", None, None)),
        check_vma=False,
    )
```

time: 147 us -> 102 us (0.69)
  Pallas kernels: 71.3 us -> 50 us
  between operations: 9.12 us -> 0.75 us
  waiting for transfers between devices: 15.1 us -> 8.18 us
  starting transfers between devices: 8.84 us -> 5.19 us
  matrix products: 6.14 us -> 4.28 us
    pallas_call x1, Pallas kernels: 29.8 us -> 19.9 us  [body(): pl.pallas_call(ascend_kernel, grid=(steps,), in_specs=[iso_spec, whole((2...]
    ppermute x3, waiting for transfers between devices: 15.1 us -> 5.59 us  [partner_2(): return lax.ppermute(block, axis, route)]
    pallas_call x1, Pallas kernels: 23.7 us -> 15.5 us  [body(): pl.pallas_call(update_kernel, grid=(steps,), in_specs=[rows_spec, whole(s...]
    pallas_call x1, Pallas kernels: 17.7 us -> 13.4 us  [body(): pl.pallas_call(gram_kernel, grid=(steps,), in_specs=[rows_spec, whole(squ...]
    ppermute x3, starting transfers between devices: 5.25 us -> 1.38 us  [partner_2(): return lax.ppermute(block, axis, route)]
    ppermute x2, waiting for transfers between devices: 0.01 us -> 2.59 us  [shifted(): return lax.ppermute(block, axis, route)]
    dot_general x3 -> x0, matrix products: 1.85 us -> none  [the longest x1 1.03 us: body(): jnp.dot(total, step, precision=highest)]
  transfers between devices with their start and end apart: 5 -> 5, of which waited for: 3 -> 3; matrix products, arithmetic and copies ran while one was open for 1% -> 1% of each run, Pallas kernels for 0% -> 13%
where the time goes in v1:
time: 102 us
  Pallas kernels  50 us (49%)
  blocking collectives  32.4 us (32%)
  waiting for transfers between devices  8.18 us (8%)
  starting transfers between devices  5.19 us (5%)
  matrix products  4.28 us (4%)
  other arithmetic  1.15 us (1%)
    pallas_call x1, Pallas kernels, body(): pl.pallas_call(ascend_kernel, grid=(steps,), in_specs=[iso_spec, whole((2...  19.9 us
    pallas_call x1, Pallas kernels, body(): pl.pallas_call(update_kernel, grid=(steps,), in_specs=[rows_spec, whole(s...  15.5 us
    all_to_all x1, blocking collectives, body(): pieces = lax.all_to_all(pieces, 'bond', 0, 0, tiled=True)  13.5 us
    pallas_call x1, Pallas kernels, body(): pl.pallas_call(gram_kernel, grid=(steps,), in_specs=[rows_spec, whole(squ...  13.4 us
    all_gather x1, blocking collectives, body(): packed = lax.all_gather(packed, 'bond', axis=0)  10.3 us
    all_gather x1, blocking collectives, body(): lax.all_gather(piece, 'bond', axis=0, tiled=True).reshape(2, *square)  8.6 us
    ppermute x3, waiting for transfers between devices, partner_2(): return lax.ppermute(block, axis, route)  5.59 us
    ppermute x2, starting transfers between devices, shifted(): return lax.ppermute(block, axis, route)  3.8 us
  transfers between devices with their start and end apart: 5, of which 3 were waited for; matrix products, arithmetic and copies ran while one was open for 1% of the time, Pallas kernels for 13%

profile of v1, /device:TPU:0, one launch (start us, length us, event | category | flops | bytes accessed | tf_op | source)
XLA Modules:
  0.0 102.0 jit_solution(5556610214579537217)
XLA Ops:
  0.6 0.0 copy-start
  0.6 1.0 %pad_maximum_fusion.edges_ref = bf16[512,256]{1,0:T(8,128)(2,1)S(1)} fusion(bf16[256,256]{1,0:T(8,128)(2,1)} %bitcast.33, bf16[256,256]{1,0:T(8,128)(2,1)} %bitcast.31), kind=kLoop, calls=%fused_computation.6 | loop fusion | flops 524288 | bytes 524288 | tf_op jit(solution)/shard_map/concatenate | solution.py:158
  1.7 0.0 copy-start.1
  1.7 19.9 %ascend.1 = (bf16[64,256,256]{2,1,0:T(8,128)(2,1)}, f32[2,256,256]{2,1,0:T(8,128)S(1)}) custom-call(bf16[256,64,256]{2,1,0:T(8,128)(2,1)} %bitcast.34, bf16[512,256]{1,0:T(8,128)(2,1)S(1)} %pad_maximum_fusion.edges_ref), custom_call_target="tpu_custom_call" | custom-call | flops 12884901888 | bytes 16777216 | tf_op jit(solution)/shard_map/ascend/pallas_call | solution.py:159
  21.6 13.5 %all_to_all.5 = f32[4,128,256]{2,1,0:T(8,128)S(1)} all-to-all(f32[4,128,256]{2,1,0:T(8,128)S(1)} %bitcast.30), channel_id=1, replica_groups=mesh['blk'=8,'bond'=4] {'bond'}, dimensions={0} | all-to-all | bytes 1048576 | tf_op jit(solution)/shard_map/all_to_all | solution.py:174
  35.1 8.6 %all_gather.9 = bf16[512,256]{1,0:T(8,128)(2,1)S(1)} all-gather(bf16[128,256]{1,0:T(8,128)(2,1)S(1)} %reduce_sum.9), channel_id=1, replica_groups=mesh['blk'=8,'bond'=4] {'bond'}, dimensions={0}, use_global_device_ids=true | all-gather | bytes 327680 | tf_op jit(solution)/shard_map/all_gather | solution.py:176
  43.7 0.1 collective-permute-start
  43.8 0.5 collective-permute-start.2
  44.4 3.3 %collective-permute-start.3 = (bf16[256,256]{1,0:T(8,128)(2,1)S(1)}, bf16[256,256]{1,0:T(8,128)(2,1)S(1)}, u32[]{:S(2)}, u32[]{:S(2)}) collective-permute-start(bf16[256,256]{1,0:T(8,128)(2,1)S(1)} %get-tuple-element.17), channel_id=1, source_target_pairs={{4,0},{8,4},{12,8},{16,12},{20,16},{24,20},{28,24},{0,28},{5,1},{9... | collective-permute-start | bytes 393224 | tf_op jit(solution)/shard_map/ppermute | solution.py:21
  47.6 0.0 collective-permute-done
  47.6 0.0 copy-done
  47.6 0.6 fusion.10
  48.2 0.6 fusion.2
  48.8 0.1 collective-permute-start.1
  48.9 1.4 %collective-permute-done.2 = bf16[256,256]{1,0:T(8,128)(2,1)S(1)} collective-permute-done((bf16[256,256]{1,0:T(8,128)(2,1)S(1)}, bf16[256,256]{1,0:T(8,128)(2,1)S(1)}, u32[]{:S(2)}, u32[]{:S(2)}) %collective-permute-start.2) | collective-permute-done | bytes 131104 | tf_op jit(solution)/shard_map/ppermute | solution.py:21
  50.3 1.2 %collective-permute-done.3 = bf16[256,256]{1,0:T(8,128)(2,1)S(1)} collective-permute-done((bf16[256,256]{1,0:T(8,128)(2,1)S(1)}, bf16[256,256]{1,0:T(8,128)(2,1)S(1)}, u32[]{:S(2)}, u32[]{:S(2)}) %collective-permute-start.3) | collective-permute-done | bytes 131104 | tf_op jit(solution)/shard_map/ppermute | solution.py:21
  51.5 0.0 copy-done.1
  51.5 0.1 add_convert_fusion.mix_ref
  51.6 5.6 %collective-permute-done.1 = f32[256,256]{1,0:T(8,128)S(1)} collective-permute-done((f32[256,256]{1,0:T(8,128)S(1)}, f32[256,256]{1,0:T(8,128)S(1)}, u32[]{:S(2)}, u32[]{:S(2)}) %collective-permute-start.1) | collective-permute-done | bytes 262176 | tf_op jit(solution)/shard_map/ppermute | solution.py:31
  57.2 0.6 fusion.7
  57.8 0.6 fusion.1
  58.4 1.2 %collective-permute-start.4 = (f32[256,256]{1,0:T(8,128)S(1)}, f32[256,256]{1,0:T(8,128)S(1)}, u32[]{:S(2)}, u32[]{:S(2)}) collective-permute-start(f32[256,256]{1,0:T(8,128)S(1)} %fusion.1), channel_id=1, source_target_pairs={{0,16},{16,0},{4,20},{20,4},{8,24},{24,8},{12,28},{28,12},{1,17},{... | collective-permute-start | bytes 786440 | tf_op jit(solution)/shard_map/ppermute | solution.py:31
  59.6 13.4 %gram.1 = (f32[256,256]{1,0:T(8,128)S(1)}, f32[256,256]{1,0:T(8,128)S(1)}, f32[256,256]{1,0:T(8,128)S(1)}) custom-call(bf16[64,256,256]{2,1,0:T(8,128)(2,1)} %get-tuple-element.9.rows_ref, bf16[256,256]{1,0:T(8,128)(2,1)S(1)} %add_convert_fusion.mix_ref), custom_call_target="tpu_custom_call" | custom-call | flops 8589934592 | bytes 8388608 | tf_op jit(solution)/shard_map/gram/pallas_call | solution.py:194
  73.0 0.0 collective-permute-done.4
  73.0 0.6 fusion.4
  73.6 1.3 %fusion.13 = (bf16[256,256]{1,0:T(8,128)(2,1)S(1)}, f32[256,256]{1,0:T(8,128)}) fusion(f32[256,256]{1,0:T(8,128)S(1)} %fusion.1, f32[256,256]{1,0:T(8,128)S(1)} %fusion.4, f32[1,256,256]{2,1,0:T(8,128)S(1)} %copy-done), kind=kOutput, calls=%fused_computation.19 | convolution fusion | flops 201523200 | bytes 1179648 | tf_op jit(solution)/shard_map/dot_general | solution.py:190
  74.9 1.3 %join.1 = bf16[272,256]{1,0:T(8,128)(2,1)S(1)} custom-call(f32[256,256]{1,0:T(8,128)S(1)} %get-tuple-element.13.self_ref, f32[256,256]{1,0:T(8,128)S(1)} %get-tuple-element.14.cross_ref, f32[256,256]{1,0:T(8,128)S(1)} %get-tuple-element.15.plain_ref, bf16[256,256]{1,0:T(8,128)(2,1)S(1)} %get-tuple-element.18.top_ref), custom_call_target="tpu_custom_call" | custom-call | tf_op jit(solution)/shard_map/join/pallas_call | solution.py:205
  76.2 10.3 %all-gather = bf16[1088,256]{1,0:T(8,128)(2,1)S(1)} all-gather(bf16[272,256]{1,0:T(8,128)(2,1)S(1)} %join.1), channel_id=2, replica_groups=mesh['blk'=8,'bond'=4] {'bond'}, dimensions={0}, use_global_device_ids=true | all-gather | bytes 696320 | tf_op jit(solution)/shard_map/all_gather | solution.py:211
  86.5 15.5 %update.1 = bf16[256,64,256]{2,1,0:T(8,128)(2,1)} custom-call(bf16[64,256,256]{2,1,0:T(8,128)(2,1)} %get-tuple-element.9.rows_ref, bf16[256,256]{1,0:T(8,128)(2,1)S(1)} %add_convert_fusion.mix_ref, bf16[256,256]{1,0:T(8,128)(2,1)S(1)} %get-tuple-element.18.top_ref, bf16[4,272,256]{2,1,0:T(8,128)(2,1)S(1)} %bitcast.29), custom_call_target="tpu_custom_call" | custom-call | flops 6442450944 | bytes 16777216 | tf_op jit(solution)/shard_map/update/pallas_call | solution.py:212
  (3 shorter events, 0.1 us)
Async XLA Ops:
  0.6 47.0 %copy-start = (f32[1,256,256]{2,1,0:T(8,128)S(1)}, f32[1,256,256]{2,1,0:T(8,128)}, u32[]{:S(2)}) copy-start(f32[1,256,256]{2,1,0:T(8,128)} %param.7) | copy-start | bytes 786436
  1.7 49.8 %copy-start.1 = (bf16[1,256,256]{2,1,0:T(8,128)(2,1)S(1)}, bf16[1,256,256]{2,1,0:T(8,128)(2,1)}, u32[]{:S(2)}) copy-start(bf16[1,256,256]{2,1,0:T(8,128)(2,1)} %param.5) | copy-start | bytes 393220
  43.7 3.9 %collective-permute-start = (f32[256,256]{1,0:T(8,128)S(1)}, f32[256,256]{1,0:T(8,128)S(1)}, u32[]{:S(2)}, u32[]{:S(2)}) collective-permute-start(f32[256,256]{1,0:T(8,128)S(1)} %convert_add_fusion), channel_id=1, source_target_pairs={{0,4},{4,0},{8,12},{12,8},{16,20},{20,16},{24,28},{28,24},{1,5},{5... | collective-permute-start | bytes 786440 | tf_op jit(solution)/shard_map/ppermute | solution.py:31
  43.8 6.5 %collective-permute-start.2 = (bf16[256,256]{1,0:T(8,128)(2,1)S(1)}, bf16[256,256]{1,0:T(8,128)(2,1)S(1)}, u32[]{:S(2)}, u32[]{:S(2)}) collective-permute-start(bf16[256,256]{1,0:T(8,128)(2,1)S(1)} %get-tuple-element.16), channel_id=1, source_target_pairs={{28,0},{0,4},{4,8},{8,12},{12,16},{16,20},{20,24},{24,28},{29,1},{... | collective-permute-start | bytes 393224 | tf_op jit(solution)/shard_map/ppermute | solution.py:21
  44.4 7.1 %collective-permute-start.3 = (bf16[256,256]{1,0:T(8,128)(2,1)S(1)}, bf16[256,256]{1,0:T(8,128)(2,1)S(1)}, u32[]{:S(2)}, u32[]{:S(2)}) collective-permute-start(bf16[256,256]{1,0:T(8,128)(2,1)S(1)} %get-tuple-element.17), channel_id=1, source_target_pairs={{4,0},{8,4},{12,8},{16,12},{20,16},{24,20},{28,24},{0,28},{5,1},{9... | collective-permute-start | bytes 393224 | tf_op jit(solution)/shard_map/ppermute | solution.py:21
  48.8 8.3 %collective-permute-start.1 = (f32[256,256]{1,0:T(8,128)S(1)}, f32[256,256]{1,0:T(8,128)S(1)}, u32[]{:S(2)}, u32[]{:S(2)}) collective-permute-start(f32[256,256]{1,0:T(8,128)S(1)} %fusion.2), channel_id=1, source_target_pairs={{0,8},{8,0},{4,12},{12,4},{16,24},{24,16},{20,28},{28,20},{1,9},{9... | collective-permute-start | bytes 786440 | tf_op jit(solution)/shard_map/ppermute | solution.py:31
  58.4 14.7 %collective-permute-start.4 = (f32[256,256]{1,0:T(8,128)S(1)}, f32[256,256]{1,0:T(8,128)S(1)}, u32[]{:S(2)}, u32[]{:S(2)}) collective-permute-start(f32[256,256]{1,0:T(8,128)S(1)} %fusion.1), channel_id=1, source_target_pairs={{0,16},{16,0},{4,20},{20,4},{8,24},{24,8},{12,28},{28,12},{1,17},{... | collective-permute-start | bytes 786440 | tf_op jit(solution)/shard_map/ppermute | solution.py:31
